TPU v7x, 32 devices: a whole 2x2x4 slice. The times are simulated.
32 devices in a mesh: row: 4 (over z), col: 8 (over y, x, core).
Axes of the slice: x: 2, y: 2, z: 4, core: 2. Of those that a mesh axis runs over, the one named last changes fastest.
Arguments:
- rhs: float32 [64, 131072], P(None, ('row', 'col')), may hold values from -6 to 6
- pivots: int32 [4096], replicated, may hold values from 0 to 131071, as said below
- factor: float32 [4096, 4, 8, 128], P('row', None, 'col'), as said below
- diag_inv: float32 [8, 512, 512], P('row'), as said below
Outputs:
- solution: float32 [64, 4, 8, 128], P(None, None, 'col')
Inputs may be any that keep to these rules, and one draw needn't show every extreme that they name: `pivots`: distinct column numbers, the first 4096 entries of a permutation of 0 .. 131071. `factor`: entry (row i, column q) is zero where q >= 512 * (i // 512). `diag_inv`: each block is unit lower triangular.
All inputs are finite; a program needn't handle non-finite values.
Results may differ from a plain program's by a relative error of at most 0.0001.
Values sent between devices are 32-bit elements; how exact they have to be, the bound alone decides.
A program may use at most 64 MiB of HBM per device.

v0:
```python
import jax
import jax.numpy as jnp
from jax import lax
from jax.sharding import PartitionSpec as P


def broadcast(shard, axis, root):
    mine = lax.axis_index(axis) == root
    return lax.psum(jnp.where(mine, shard, jnp.zeros_like(shard)), axis)


def apply_inverse(values, block_inv):
    return lax.dot_general(
        values,
        block_inv,
        (((1,), (1,)), ((), ())),
        precision=lax.Precision.HIGHEST,
        preferred_element_type=jnp.float32,
    )


def per_device(rhs, pivots, factor, diag_inv):
    my_row = lax.axis_index("row")
    my_col = lax.axis_index("col")
    col_count = lax.axis_size("col")
    rhs_count = rhs.shape[0]
    slab_rows = factor.shape[0]
    rounds = factor.shape[1]
    piece_len = factor.shape[3]
    block_len = diag_inv.shape[1]
    pieces = block_len // piece_len
    blocks_here = slab_rows // block_len
    total_blocks = blocks_here * lax.axis_size("row")
    first_column = (my_row * col_count + my_col) * rhs.shape[1]
    source_len = rhs.shape[1]
    located = pivots - first_column
    inside = (located >= 0) & (located < source_len)
    taken = jnp.take(rhs, jnp.clip(located, 0, source_len - 1), axis=1)
    taken = jnp.where(inside[None, :], taken, 0.0)
    permuted = lax.psum_scatter(
        jnp.transpose(
            taken.reshape(rhs_count, blocks_here * lax.axis_size("row"), block_len), (1, 0, 2)
        ),
        "row",
        scatter_dimension=0,
        tiled=True,
    )
    permuted = lax.psum(permuted, "col")
    factor_rows = factor.reshape(slab_rows, rounds * piece_len)

    def advance(number, solved):
        owner_row = number // blocks_here
        local_block = number % blocks_here
        block_rows = lax.dynamic_slice_in_dim(factor_rows, local_block * block_len, block_len, 0)
        partial_value = lax.dot_general(
            solved.reshape(rhs_count, rounds * piece_len),
            block_rows,
            (((1,), (1,)), ((), ())),
            precision=lax.Precision.HIGHEST,
            preferred_element_type=jnp.float32,
        )
        own_rhs = lax.dynamic_index_in_dim(permuted, local_block, 0, keepdims=False)
        block_inv = lax.dynamic_index_in_dim(diag_inv, local_block, 0, keepdims=False)
        summed = lax.psum(partial_value, "col")
        fresh = apply_inverse(own_rhs - summed, block_inv)
        fresh = broadcast(fresh, "row", owner_row)
        first_piece = number * pieces
        offset_piece = (my_col - first_piece) % col_count
        owns = offset_piece < pieces
        which = jnp.clip(offset_piece, 0, pieces - 1)
        local_round = jnp.clip((first_piece + offset_piece) // col_count, 0, rounds - 1)
        piece = lax.dynamic_slice_in_dim(fresh, which * piece_len, piece_len, 1)
        updated = lax.dynamic_update_index_in_dim(solved, piece[:, None, :], local_round, 1)
        return jnp.where(owns, updated, solved)

    start_state = jnp.zeros((rhs_count, rounds, 1, piece_len), jnp.float32)
    return lax.fori_loop(0, total_blocks, advance, start_state)


def solution(mesh):
    return jax.shard_map(
        per_device,
        mesh=mesh,
        in_specs=(P(None, ("row", "col")), P(), P("row", None, "col", None), P("row", None, None)),
        out_specs=P(None, None, "col", None),
        check_vma=False,
    )
```

profile of v0, /device:TPU:0, one launch (start us, length us, event | category | flops | bytes accessed | tf_op | source)
XLA Modules:
  0.0 882.2 jit_solution(17491685887215917001)
XLA Ops:
  9.9 14.1 %gather_fusion = f32[4096,64]{1,0:T(8,128)} fusion(f32[64,4096]{0,1:T(8,128)S(1)} %copy.8, s32[4096]{0:T(1024)S(1)} %fusion.8), kind=kCustom, calls=%fused_computation | custom fusion | bytes 2113536 | tf_op jit(solution)/shard_map/jit(_take)/gather | solution.py:38
  27.4 30.1 %reduce-scatter.2.cloned.1.call-done = f32[2,64,512]{2,1,0:T(8,128)} async-done(((f32[8,64,512]{2,1,0:T(8,128)}), f32[2,64,512]{2,1,0:T(8,128)}) %reduce-scatter.2.cloned.1.call-update) | async-done | bytes 262160 | tf_op jit(solution)/shard_map/reduce_scatter | solution.py:40
  59.3 53.7 %all-reduce.4.cloned.1.call-done = f32[2,64,512]{2,1,0:T(8,128)} async-done(((f32[2,64,512]{2,1,0:T(8,128)}), f32[2,64,512]{2,1,0:T(8,128)}) %all-reduce.4.cloned.1.call-update) | async-done | bytes 262160 | tf_op jit(solution)/shard_map/psum | solution.py:48
  113.0 761.7 %while.16 = (s32[]{:T(128)}, f32[64,4,1,128]{3,1,0,2:T(4,128)S(1)}, s32[]{:T(128)}, f32[2,64,512]{2,1,0:T(8,128)}, f32[1024,512]{1,0:T(8,128)S(1)}, /*index=5*/f...) while((s32[]{:T(128)}, f32[64,4,1,128]{3,1,0,2:T(4,128)S(1)}, ...), condition=%wide.region_5.6_spmd, body=%wide.region_2.5_spmd.sunk | while | flops 402792448 | bytes 4557184 | solution.py:77
  115.0 54.8 %all-reduce.6.cloned.1.call-done = f32[64,512]{1,0:T(8,128)} async-done(((f32[64,512]{1,0:T(8,128)}), f32[64,512]{1,0:T(8,128)}) %all-reduce.6.cloned.1.call-update) | async-done | bytes 131088 | tf_op jit(solution)/shard_map/while/body/eval_jaxpr/psum | solution.py:64
  169.7 3.1 convolution_select_fusion.2
  172.9 34.1 %all-reduce.8.cloned.1.call-done = f32[64,512]{1,0:T(8,128)} async-done(((f32[64,512]{1,0:T(8,128)}), f32[64,512]{1,0:T(8,128)}) %all-reduce.8.cloned.1.call-update) | async-done | bytes 131088 | tf_op jit(solution)/shard_map/while/body/eval_jaxpr/psum | solution.py:9
  210.0 54.8 %all-reduce.6.cloned.1.call-done = f32[64,512]{1,0:T(8,128)} async-done(((f32[64,512]{1,0:T(8,128)}), f32[64,512]{1,0:T(8,128)}) %all-reduce.6.cloned.1.call-update) | async-done | bytes 131088 | tf_op jit(solution)/shard_map/while/body/eval_jaxpr/psum | solution.py:64
  268.0 34.1 %all-reduce.8.cloned.1.call-done = f32[64,512]{1,0:T(8,128)} async-done(((f32[64,512]{1,0:T(8,128)}), f32[64,512]{1,0:T(8,128)}) %all-reduce.8.cloned.1.call-update) | async-done | bytes 131088 | tf_op jit(solution)/shard_map/while/body/eval_jaxpr/psum | solution.py:9
  305.1 55.1 %all-reduce.6.cloned.1.call-done = f32[64,512]{1,0:T(8,128)} async-done(((f32[64,512]{1,0:T(8,128)}), f32[64,512]{1,0:T(8,128)}) %all-reduce.6.cloned.1.call-update) | async-done | bytes 131088 | tf_op jit(solution)/shard_map/while/body/eval_jaxpr/psum | solution.py:64
  363.3 34.1 %all-reduce.8.cloned.1.call-done = f32[64,512]{1,0:T(8,128)} async-done(((f32[64,512]{1,0:T(8,128)}), f32[64,512]{1,0:T(8,128)}) %all-reduce.8.cloned.1.call-update) | async-done | bytes 131088 | tf_op jit(solution)/shard_map/while/body/eval_jaxpr/psum | solution.py:9
  400.4 55.1 %all-reduce.6.cloned.1.call-done = f32[64,512]{1,0:T(8,128)} async-done(((f32[64,512]{1,0:T(8,128)}), f32[64,512]{1,0:T(8,128)}) %all-reduce.6.cloned.1.call-update) | async-done | bytes 131088 | tf_op jit(solution)/shard_map/while/body/eval_jaxpr/psum | solution.py:64
  455.5 3.1 convolution_select_fusion.2
  458.7 34.1 %all-reduce.8.cloned.1.call-done = f32[64,512]{1,0:T(8,128)} async-done(((f32[64,512]{1,0:T(8,128)}), f32[64,512]{1,0:T(8,128)}) %all-reduce.8.cloned.1.call-update) | async-done | bytes 131088 | tf_op jit(solution)/shard_map/while/body/eval_jaxpr/psum | solution.py:9
  495.8 55.1 %all-reduce.6.cloned.1.call-done = f32[64,512]{1,0:T(8,128)} async-done(((f32[64,512]{1,0:T(8,128)}), f32[64,512]{1,0:T(8,128)}) %all-reduce.6.cloned.1.call-update) | async-done | bytes 131088 | tf_op jit(solution)/shard_map/while/body/eval_jaxpr/psum | solution.py:64
  554.1 34.1 %all-reduce.8.cloned.1.call-done = f32[64,512]{1,0:T(8,128)} async-done(((f32[64,512]{1,0:T(8,128)}), f32[64,512]{1,0:T(8,128)}) %all-reduce.8.cloned.1.call-update) | async-done | bytes 131088 | tf_op jit(solution)/shard_map/while/body/eval_jaxpr/psum | solution.py:9
  591.1 55.1 %all-reduce.6.cloned.1.call-done = f32[64,512]{1,0:T(8,128)} async-done(((f32[64,512]{1,0:T(8,128)}), f32[64,512]{1,0:T(8,128)}) %all-reduce.6.cloned.1.call-update) | async-done | bytes 131088 | tf_op jit(solution)/shard_map/while/body/eval_jaxpr/psum | solution.py:64
  646.2 3.1 convolution_select_fusion.2
  649.4 34.1 %all-reduce.8.cloned.1.call-done = f32[64,512]{1,0:T(8,128)} async-done(((f32[64,512]{1,0:T(8,128)}), f32[64,512]{1,0:T(8,128)}) %all-reduce.8.cloned.1.call-update) | async-done | bytes 131088 | tf_op jit(solution)/shard_map/while/body/eval_jaxpr/psum | solution.py:9
  686.5 54.8 %all-reduce.6.cloned.1.call-done = f32[64,512]{1,0:T(8,128)} async-done(((f32[64,512]{1,0:T(8,128)}), f32[64,512]{1,0:T(8,128)}) %all-reduce.6.cloned.1.call-update) | async-done | bytes 131088 | tf_op jit(solution)/shard_map/while/body/eval_jaxpr/psum | solution.py:64
  741.3 3.1 convolution_select_fusion.2
  744.5 34.1 %all-reduce.8.cloned.1.call-done = f32[64,512]{1,0:T(8,128)} async-done(((f32[64,512]{1,0:T(8,128)}), f32[64,512]{1,0:T(8,128)}) %all-reduce.8.cloned.1.call-update) | async-done | bytes 131088 | tf_op jit(solution)/shard_map/while/body/eval_jaxpr/psum | solution.py:9
  781.6 54.8 %all-reduce.6.cloned.1.call-done = f32[64,512]{1,0:T(8,128)} async-done(((f32[64,512]{1,0:T(8,128)}), f32[64,512]{1,0:T(8,128)}) %all-reduce.6.cloned.1.call-update) | async-done | bytes 131088 | tf_op jit(solution)/shard_map/while/body/eval_jaxpr/psum | solution.py:64
  839.5 34.1 %all-reduce.8.cloned.1.call-done = f32[64,512]{1,0:T(8,128)} async-done(((f32[64,512]{1,0:T(8,128)}), f32[64,512]{1,0:T(8,128)}) %all-reduce.8.cloned.1.call-update) | async-done | bytes 131088 | tf_op jit(solution)/shard_map/while/body/eval_jaxpr/psum | solution.py:9
  (83 shorter events, 44.9 us)
Async XLA Ops:
  6.5 51.0 %reduce-scatter.2.cloned.1.call-start = ((), (), s32[]{:S(2)}) async-start(), calls=%async_computation.1 | async-start | bytes 1310720 | tf_op jit(solution)/shard_map/reduce_scatter | solution.py:40
  27.3 85.6 %all-reduce.4.cloned.1.call-start = ((), (), s32[]{:S(2)}) async-start(), calls=%async_computation.2 | async-start | bytes 524288 | tf_op jit(solution)/shard_map/psum | solution.py:48
  113.0 56.7 %all-reduce.6.cloned.1.call-start = ((), (), s32[]{:S(2)}) async-start(), calls=%async_computation.3 | async-start | bytes 262144 | tf_op jit(solution)/shard_map/while/body/eval_jaxpr/psum | solution.py:64
  114.9 92.2 %all-reduce.8.cloned.1.call-start = ((), (), s32[]{:S(2)}) async-start(), calls=%async_computation.4 | async-start | bytes 262144 | tf_op jit(solution)/shard_map/while/body/eval_jaxpr/psum | solution.py:9
  208.1 56.7 %all-reduce.6.cloned.1.call-start = ((), (), s32[]{:S(2)}) async-start(), calls=%async_computation.3 | async-start | bytes 262144 | tf_op jit(solution)/shard_map/while/body/eval_jaxpr/psum | solution.py:64
  209.9 92.2 %all-reduce.8.cloned.1.call-start = ((), (), s32[]{:S(2)}) async-start(), calls=%async_computation.4 | async-start | bytes 262144 | tf_op jit(solution)/shard_map/while/body/eval_jaxpr/psum | solution.py:9
  303.1 57.0 %all-reduce.6.cloned.1.call-start = ((), (), s32[]{:S(2)}) async-start(), calls=%async_computation.3 | async-start | bytes 262144 | tf_op jit(solution)/shard_map/while/body/eval_jaxpr/psum | solution.py:64
  305.0 92.5 %all-reduce.8.cloned.1.call-start = ((), (), s32[]{:S(2)}) async-start(), calls=%async_computation.4 | async-start | bytes 262144 | tf_op jit(solution)/shard_map/while/body/eval_jaxpr/psum | solution.py:9
  398.5 57.0 %all-reduce.6.cloned.1.call-start = ((), (), s32[]{:S(2)}) async-start(), calls=%async_computation.3 | async-start | bytes 262144 | tf_op jit(solution)/shard_map/while/body/eval_jaxpr/psum | solution.py:64
  400.4 92.5 %all-reduce.8.cloned.1.call-start = ((), (), s32[]{:S(2)}) async-start(), calls=%async_computation.4 | async-start | bytes 262144 | tf_op jit(solution)/shard_map/while/body/eval_jaxpr/psum | solution.py:9
  493.8 57.0 %all-reduce.6.cloned.1.call-start = ((), (), s32[]{:S(2)}) async-start(), calls=%async_computation.3 | async-start | bytes 262144 | tf_op jit(solution)/shard_map/while/body/eval_jaxpr/psum | solution.py:64
  495.7 92.5 %all-reduce.8.cloned.1.call-start = ((), (), s32[]{:S(2)}) async-start(), calls=%async_computation.4 | async-start | bytes 262144 | tf_op jit(solution)/shard_map/while/body/eval_jaxpr/psum | solution.py:9
  589.2 57.0 %all-reduce.6.cloned.1.call-start = ((), (), s32[]{:S(2)}) async-start(), calls=%async_computation.3 | async-start | bytes 262144 | tf_op jit(solution)/shard_map/while/body/eval_jaxpr/psum | solution.py:64
  591.1 92.5 %all-reduce.8.cloned.1.call-start = ((), (), s32[]{:S(2)}) async-start(), calls=%async_computation.4 | async-start | bytes 262144 | tf_op jit(solution)/shard_map/while/body/eval_jaxpr/psum | solution.py:9
  684.6 56.7 %all-reduce.6.cloned.1.call-start = ((), (), s32[]{:S(2)}) async-start(), calls=%async_computation.3 | async-start | bytes 262144 | tf_op jit(solution)/shard_map/while/body/eval_jaxpr/psum | solution.py:64
  686.4 92.2 %all-reduce.8.cloned.1.call-start = ((), (), s32[]{:S(2)}) async-start(), calls=%async_computation.4 | async-start | bytes 262144 | tf_op jit(solution)/shard_map/while/body/eval_jaxpr/psum | solution.py:9
  779.6 56.7 %all-reduce.6.cloned.1.call-start = ((), (), s32[]{:S(2)}) async-start(), calls=%async_computation.3 | async-start | bytes 262144 | tf_op jit(solution)/shard_map/while/body/eval_jaxpr/psum | solution.py:64
  781.5 92.2 %all-reduce.8.cloned.1.call-start = ((), (), s32[]{:S(2)}) async-start(), calls=%async_computation.4 | async-start | bytes 262144 | tf_op jit(solution)/shard_map/while/body/eval_jaxpr/psum | solution.py:9
  874.7 0.7 copy-start
Sparse Core Ops, SparseCore 0:
  27.5 29.9 reduce-scatter.1
  60.5 52.3 all-reduce.3
  116.8 52.8 all-reduce.5
  173.0 34.0 all-reduce.7
  211.6 53.1 all-reduce.5
  268.0 34.0 all-reduce.7
  307.0 53.1 all-reduce.5
  363.4 34.0 all-reduce.7
  402.3 53.1 all-reduce.5
  458.8 34.0 all-reduce.7
  497.7 53.1 all-reduce.5
  554.1 34.0 all-reduce.7
  593.0 53.1 all-reduce.5
  649.5 34.0 all-reduce.7
  688.1 53.1 all-reduce.5
  744.6 34.0 all-reduce.7
  783.2 53.1 all-reduce.5
  839.6 34.0 all-reduce.7
where the time goes:
time: 883 us; the launch traced here: 882 us
  waiting for transfers between devices  796 us (90%)
  matrix products  39.5 us (4%)
  local copies, waits for them, and re-layouts  28 us (3%)
  between operations  13.5 us (2%)
    psum x8, waiting for transfers between devices, advance(): summed = lax.psum(partial_value, 'col')  439 us
    psum x8, waiting for transfers between devices, broadcast(): return lax.psum(jnp.where(mine, shard, jnp.zeros_like(shard)), axis)  273 us
    psum x1, waiting for transfers between devices, per_device(): permuted = lax.psum(permuted, 'col')  53.7 us
    reduce_scatter x1, waiting for transfers between devices, per_device(): lax.psum_scatter(jnp.transpose(taken.reshape(rhs_count, blocks_here * lax...  30.1 us
    dot_general x8, matrix products, apply_inverse(): lax.dot_general(values, block_inv, (((1,), (1,)), ((), ())), precision=la...  25.1 us
  transfers between devices with their start and end apart: 18, of which 18 were waited for; matrix products, arithmetic and copies ran while one was open for 0% of the time, Pallas kernels for 0%

commit v1 on v0

--- a/solution.py
+++ b/solution.py
@@ -61,7 +61,7 @@
         )
         own_rhs = lax.dynamic_index_in_dim(permuted, local_block, 0, keepdims=False)
         block_inv = lax.dynamic_index_in_dim(diag_inv, local_block, 0, keepdims=False)
-        summed = lax.psum(partial_value, "col")
+        summed = jnp.sum(lax.all_gather(partial_value, "col"), axis=0)
         fresh = apply_inverse(own_rhs - summed, block_inv)
         fresh = broadcast(fresh, "row", owner_row)
         first_piece = number * pieces

time: 883 us -> 648 us (0.73)
  waiting for transfers between devices: 796 us -> 551 us
  other arithmetic: 3 us -> 13.5 us
    psum x8 -> x0, waiting for transfers between devices: 439 us -> none  [advance(): summed = lax.psum(partial_value, 'col')]
    all_gather x0 -> x8, waiting for transfers between devices: none -> 189 us  [advance(): summed = jnp.sum(lax.all_gather(partial_value, 'col'), axis=0)]
    reduce_sum x0 -> x8, other arithmetic: none -> 10.5 us  [advance(): summed = jnp.sum(lax.all_gather(partial_value, 'col'), axis=0)]
where the time goes in v1:
time: 648 us; the launch traced here: 647 us
  waiting for transfers between devices  551 us (85%)
  matrix products  38.4 us (6%)
  local copies, waits for them, and re-layouts  28.1 us (4%)
  other arithmetic  13.5 us (2%)
  between operations  13.5 us (2%)
    psum x8, waiting for transfers between devices, broadcast(): return lax.psum(jnp.where(mine, shard, jnp.zeros_like(shard)), axis)  278 us
    all_gather x8, waiting for transfers between devices, advance(): summed = jnp.sum(lax.all_gather(partial_value, 'col'), axis=0)  189 us
    psum x1, waiting for transfers between devices, per_device(): permuted = lax.psum(permuted, 'col')  53.7 us
    reduce_scatter x1, waiting for transfers between devices, per_device(): lax.psum_scatter(jnp.transpose(taken.reshape(rhs_count, blocks_here * lax...  30.1 us
    dot_general x8, matrix products, apply_inverse(): lax.dot_general(values, block_inv, (((1,), (1,)), ((), ())), precision=la...  23.9 us
    gather x2, local copies, waits for them, and re-layouts, per_device(): taken = jnp.take(rhs, jnp.clip(located, 0, source_len - 1), axis=1)  16.3 us
    dot_general x8, matrix products, advance(): lax.dot_general(solved.reshape(rhs_count, rounds * piece_len), block_rows...  14.4 us
  transfers between devices with their start and end apart: 18, of which 18 were waited for; matrix products, arithmetic and copies ran while one was open for 0% of the time, Pallas kernels for 0%

profile of v1, /device:TPU:0, one launch (start us, length us, event | category | flops | bytes accessed | tf_op | source)
XLA Modules:
  0.0 646.8 jit_solution(2511851599516030363)
XLA Ops:
  9.9 14.2 %gather_fusion = f32[4096,64]{1,0:T(8,128)} fusion(f32[64,4096]{0,1:T(8,128)S(1)} %copy.8, s32[4096]{0:T(1024)S(1)} %fusion.9), kind=kCustom, calls=%fused_computation | custom fusion | bytes 2113536 | tf_op jit(solution)/shard_map/jit(_take)/gather | solution.py:38
  27.5 30.1 %reduce-scatter.2.cloned.1.call-done = f32[2,64,512]{2,1,0:T(8,128)} async-done(((f32[8,64,512]{2,1,0:T(8,128)}), f32[2,64,512]{2,1,0:T(8,128)}) %reduce-scatter.2.cloned.1.call-update) | async-done | bytes 262160 | tf_op jit(solution)/shard_map/reduce_scatter | solution.py:40
  59.4 53.7 %all-reduce.3.cloned.1.call-done = f32[2,64,512]{2,1,0:T(8,128)} async-done(((f32[2,64,512]{2,1,0:T(8,128)}), f32[2,64,512]{2,1,0:T(8,128)}) %all-reduce.3.cloned.1.call-update) | async-done | bytes 262160 | tf_op jit(solution)/shard_map/psum | solution.py:48
  113.1 526.2 %while.16 = (s32[]{:T(128)}, f32[64,4,1,128]{3,1,0,2:T(4,128)S(1)}, s32[]{:T(128)}, f32[2,64,512]{2,1,0:T(8,128)}, f32[1024,512]{1,0:T(8,128)S(1)}, /*index=5*/f...) while((s32[]{:T(128)}, f32[64,4,1,128]{3,1,0,2:T(4,128)S(1)}, ...), condition=%wide.region_5.6_spmd, body=%wide.region_2.5_spmd.sunk | while | flops 402989056 | bytes 9537960 | solution.py:77
  115.1 23.5 %all-gather.5.cloned.1.call-done = f32[512,512]{1,0:T(8,128)} async-done(((f32[64,512]{1,0:T(8,128)}), f32[512,512]{1,0:T(8,128)}) %all-gather.5.cloned.1.call-update) | async-done | bytes 1048592 | tf_op jit(solution)/shard_map/while/body/eval_jaxpr/all_gather | solution.py:64
  143.0 34.7 %all-reduce.5.cloned.1.call-done = f32[64,512]{1,0:T(8,128)} async-done(((f32[64,512]{1,0:T(8,128)}), f32[64,512]{1,0:T(8,128)}) %all-reduce.5.cloned.1.call-update) | async-done | bytes 131088 | tf_op jit(solution)/shard_map/while/body/eval_jaxpr/psum | solution.py:9
  180.7 23.5 %all-gather.5.cloned.1.call-done = f32[512,512]{1,0:T(8,128)} async-done(((f32[64,512]{1,0:T(8,128)}), f32[512,512]{1,0:T(8,128)}) %all-gather.5.cloned.1.call-update) | async-done | bytes 1048592 | tf_op jit(solution)/shard_map/while/body/eval_jaxpr/all_gather | solution.py:64
  208.6 34.7 %all-reduce.5.cloned.1.call-done = f32[64,512]{1,0:T(8,128)} async-done(((f32[64,512]{1,0:T(8,128)}), f32[64,512]{1,0:T(8,128)}) %all-reduce.5.cloned.1.call-update) | async-done | bytes 131088 | tf_op jit(solution)/shard_map/while/body/eval_jaxpr/psum | solution.py:9
  246.3 23.8 %all-gather.5.cloned.1.call-done = f32[512,512]{1,0:T(8,128)} async-done(((f32[64,512]{1,0:T(8,128)}), f32[512,512]{1,0:T(8,128)}) %all-gather.5.cloned.1.call-update) | async-done | bytes 1048592 | tf_op jit(solution)/shard_map/while/body/eval_jaxpr/all_gather | solution.py:64
  274.5 34.7 %all-reduce.5.cloned.1.call-done = f32[64,512]{1,0:T(8,128)} async-done(((f32[64,512]{1,0:T(8,128)}), f32[64,512]{1,0:T(8,128)}) %all-reduce.5.cloned.1.call-update) | async-done | bytes 131088 | tf_op jit(solution)/shard_map/while/body/eval_jaxpr/psum | solution.py:9
  312.2 23.8 %all-gather.5.cloned.1.call-done = f32[512,512]{1,0:T(8,128)} async-done(((f32[64,512]{1,0:T(8,128)}), f32[512,512]{1,0:T(8,128)}) %all-gather.5.cloned.1.call-update) | async-done | bytes 1048592 | tf_op jit(solution)/shard_map/while/body/eval_jaxpr/all_gather | solution.py:64
  337.4 3.0 convolution_select_fusion.2
  340.5 34.7 %all-reduce.5.cloned.1.call-done = f32[64,512]{1,0:T(8,128)} async-done(((f32[64,512]{1,0:T(8,128)}), f32[64,512]{1,0:T(8,128)}) %all-reduce.5.cloned.1.call-update) | async-done | bytes 131088 | tf_op jit(solution)/shard_map/while/body/eval_jaxpr/psum | solution.py:9
  378.2 23.8 %all-gather.5.cloned.1.call-done = f32[512,512]{1,0:T(8,128)} async-done(((f32[64,512]{1,0:T(8,128)}), f32[512,512]{1,0:T(8,128)}) %all-gather.5.cloned.1.call-update) | async-done | bytes 1048592 | tf_op jit(solution)/shard_map/while/body/eval_jaxpr/all_gather | solution.py:64
  403.3 3.0 convolution_select_fusion.2
  406.4 34.7 %all-reduce.5.cloned.1.call-done = f32[64,512]{1,0:T(8,128)} async-done(((f32[64,512]{1,0:T(8,128)}), f32[64,512]{1,0:T(8,128)}) %all-reduce.5.cloned.1.call-update) | async-done | bytes 131088 | tf_op jit(solution)/shard_map/while/body/eval_jaxpr/psum | solution.py:9
  444.1 23.8 %all-gather.5.cloned.1.call-done = f32[512,512]{1,0:T(8,128)} async-done(((f32[64,512]{1,0:T(8,128)}), f32[512,512]{1,0:T(8,128)}) %all-gather.5.cloned.1.call-update) | async-done | bytes 1048592 | tf_op jit(solution)/shard_map/while/body/eval_jaxpr/all_gather | solution.py:64
  472.3 34.7 %all-reduce.5.cloned.1.call-done = f32[64,512]{1,0:T(8,128)} async-done(((f32[64,512]{1,0:T(8,128)}), f32[64,512]{1,0:T(8,128)}) %all-reduce.5.cloned.1.call-update) | async-done | bytes 131088 | tf_op jit(solution)/shard_map/while/body/eval_jaxpr/psum | solution.py:9
  510.0 23.5 %all-gather.5.cloned.1.call-done = f32[512,512]{1,0:T(8,128)} async-done(((f32[64,512]{1,0:T(8,128)}), f32[512,512]{1,0:T(8,128)}) %all-gather.5.cloned.1.call-update) | async-done | bytes 1048592 | tf_op jit(solution)/shard_map/while/body/eval_jaxpr/all_gather | solution.py:64
  534.9 3.0 convolution_select_fusion.2
  537.9 34.7 %all-reduce.5.cloned.1.call-done = f32[64,512]{1,0:T(8,128)} async-done(((f32[64,512]{1,0:T(8,128)}), f32[64,512]{1,0:T(8,128)}) %all-reduce.5.cloned.1.call-update) | async-done | bytes 131088 | tf_op jit(solution)/shard_map/while/body/eval_jaxpr/psum | solution.py:9
  575.7 23.5 %all-gather.5.cloned.1.call-done = f32[512,512]{1,0:T(8,128)} async-done(((f32[64,512]{1,0:T(8,128)}), f32[512,512]{1,0:T(8,128)}) %all-gather.5.cloned.1.call-update) | async-done | bytes 1048592 | tf_op jit(solution)/shard_map/while/body/eval_jaxpr/all_gather | solution.py:64
  600.5 3.0 convolution_select_fusion.2
  603.6 34.7 %all-reduce.5.cloned.1.call-done = f32[64,512]{1,0:T(8,128)} async-done(((f32[64,512]{1,0:T(8,128)}), f32[64,512]{1,0:T(8,128)}) %all-reduce.5.cloned.1.call-update) | async-done | bytes 131088 | tf_op jit(solution)/shard_map/while/body/eval_jaxpr/psum | solution.py:9
  (107 shorter events, 54.8 us)
Async XLA Ops:
  6.5 51.1 %reduce-scatter.2.cloned.1.call-start = ((), (), s32[]{:S(2)}) async-start(), calls=%async_computation.1 | async-start | bytes 1310720 | tf_op jit(solution)/shard_map/reduce_scatter | solution.py:40
  27.4 85.6 %all-reduce.3.cloned.1.call-start = ((), (), s32[]{:S(2)}) async-start(), calls=%async_computation.2 | async-start | bytes 524288 | tf_op jit(solution)/shard_map/psum | solution.py:48
  113.1 26.8 %copy-start.1 = (f32[2,64,512]{2,1,0:T(8,128)S(1)}, f32[2,64,512]{2,1,0:T(8,128)}, u32[]{:S(2)}) copy-start(f32[2,64,512]{2,1,0:T(8,128)} %get-tuple-element.288) | copy-start | bytes 786436 | tf_op jit(solution)/shard_map/while
  113.1 25.5 %all-gather.5.cloned.1.call-start = ((), (), s32[]{:S(2)}) async-start(), calls=%async_computation.3 | async-start | bytes 1179648 | tf_op jit(solution)/shard_map/while/body/eval_jaxpr/all_gather | solution.py:64
  115.0 62.7 %all-reduce.5.cloned.1.call-start = ((), (), s32[]{:S(2)}) async-start(), calls=%async_computation.4 | async-start | bytes 262144 | tf_op jit(solution)/shard_map/while/body/eval_jaxpr/psum | solution.py:9
  178.7 25.5 %all-gather.5.cloned.1.call-start = ((), (), s32[]{:S(2)}) async-start(), calls=%async_computation.3 | async-start | bytes 1179648 | tf_op jit(solution)/shard_map/while/body/eval_jaxpr/all_gather | solution.py:64
  180.6 62.7 %all-reduce.5.cloned.1.call-start = ((), (), s32[]{:S(2)}) async-start(), calls=%async_computation.4 | async-start | bytes 262144 | tf_op jit(solution)/shard_map/while/body/eval_jaxpr/psum | solution.py:9
  244.3 27.1 %copy-start.1 = (f32[2,64,512]{2,1,0:T(8,128)S(1)}, f32[2,64,512]{2,1,0:T(8,128)}, u32[]{:S(2)}) copy-start(f32[2,64,512]{2,1,0:T(8,128)} %get-tuple-element.288) | copy-start | bytes 786436 | tf_op jit(solution)/shard_map/while
  244.4 25.8 %all-gather.5.cloned.1.call-start = ((), (), s32[]{:S(2)}) async-start(), calls=%async_computation.3 | async-start | bytes 1179648 | tf_op jit(solution)/shard_map/while/body/eval_jaxpr/all_gather | solution.py:64
  246.2 63.0 %all-reduce.5.cloned.1.call-start = ((), (), s32[]{:S(2)}) async-start(), calls=%async_computation.4 | async-start | bytes 262144 | tf_op jit(solution)/shard_map/while/body/eval_jaxpr/psum | solution.py:9
  310.3 27.1 %copy-start.1 = (f32[2,64,512]{2,1,0:T(8,128)S(1)}, f32[2,64,512]{2,1,0:T(8,128)}, u32[]{:S(2)}) copy-start(f32[2,64,512]{2,1,0:T(8,128)} %get-tuple-element.288) | copy-start | bytes 786436 | tf_op jit(solution)/shard_map/while
  310.3 25.8 %all-gather.5.cloned.1.call-start = ((), (), s32[]{:S(2)}) async-start(), calls=%async_computation.3 | async-start | bytes 1179648 | tf_op jit(solution)/shard_map/while/body/eval_jaxpr/all_gather | solution.py:64
  312.2 63.0 %all-reduce.5.cloned.1.call-start = ((), (), s32[]{:S(2)}) async-start(), calls=%async_computation.4 | async-start | bytes 262144 | tf_op jit(solution)/shard_map/while/body/eval_jaxpr/psum | solution.py:9
  376.2 27.1 %copy-start.1 = (f32[2,64,512]{2,1,0:T(8,128)S(1)}, f32[2,64,512]{2,1,0:T(8,128)}, u32[]{:S(2)}) copy-start(f32[2,64,512]{2,1,0:T(8,128)} %get-tuple-element.288) | copy-start | bytes 786436 | tf_op jit(solution)/shard_map/while
  376.2 25.8 %all-gather.5.cloned.1.call-start = ((), (), s32[]{:S(2)}) async-start(), calls=%async_computation.3 | async-start | bytes 1179648 | tf_op jit(solution)/shard_map/while/body/eval_jaxpr/all_gather | solution.py:64
  378.1 63.0 %all-reduce.5.cloned.1.call-start = ((), (), s32[]{:S(2)}) async-start(), calls=%async_computation.4 | async-start | bytes 262144 | tf_op jit(solution)/shard_map/while/body/eval_jaxpr/psum | solution.py:9
  442.1 27.1 %copy-start.1 = (f32[2,64,512]{2,1,0:T(8,128)S(1)}, f32[2,64,512]{2,1,0:T(8,128)}, u32[]{:S(2)}) copy-start(f32[2,64,512]{2,1,0:T(8,128)} %get-tuple-element.288) | copy-start | bytes 786436 | tf_op jit(solution)/shard_map/while
  442.1 25.8 %all-gather.5.cloned.1.call-start = ((), (), s32[]{:S(2)}) async-start(), calls=%async_computation.3 | async-start | bytes 1179648 | tf_op jit(solution)/shard_map/while/body/eval_jaxpr/all_gather | solution.py:64
  444.0 63.0 %all-reduce.5.cloned.1.call-start = ((), (), s32[]{:S(2)}) async-start(), calls=%async_computation.4 | async-start | bytes 262144 | tf_op jit(solution)/shard_map/while/body/eval_jaxpr/psum | solution.py:9
  508.1 26.8 %copy-start.1 = (f32[2,64,512]{2,1,0:T(8,128)S(1)}, f32[2,64,512]{2,1,0:T(8,128)}, u32[]{:S(2)}) copy-start(f32[2,64,512]{2,1,0:T(8,128)} %get-tuple-element.288) | copy-start | bytes 786436 | tf_op jit(solution)/shard_map/while
  508.1 25.5 %all-gather.5.cloned.1.call-start = ((), (), s32[]{:S(2)}) async-start(), calls=%async_computation.3 | async-start | bytes 1179648 | tf_op jit(solution)/shard_map/while/body/eval_jaxpr/all_gather | solution.py:64
  510.0 62.7 %all-reduce.5.cloned.1.call-start = ((), (), s32[]{:S(2)}) async-start(), calls=%async_computation.4 | async-start | bytes 262144 | tf_op jit(solution)/shard_map/while/body/eval_jaxpr/psum | solution.py:9
  573.7 25.5 %all-gather.5.cloned.1.call-start = ((), (), s32[]{:S(2)}) async-start(), calls=%async_computation.3 | async-start | bytes 1179648 | tf_op jit(solution)/shard_map/while/body/eval_jaxpr/all_gather | solution.py:64
  575.6 62.7 %all-reduce.5.cloned.1.call-start = ((), (), s32[]{:S(2)}) async-start(), calls=%async_computation.4 | async-start | bytes 262144 | tf_op jit(solution)/shard_map/while/body/eval_jaxpr/psum | solution.py:9
  (3 other events, 54.3 us)
Sparse Core Ops, SparseCore 0:
  27.6 29.9 reduce-scatter.1
  60.6 52.3 all-reduce.2
  115.8 22.7 all-gather.4
  143.1 34.6 all-reduce.4
  181.1 23.0 all-gather.4
  208.7 34.6 all-reduce.4
  247.1 23.0 all-gather.4
  274.6 34.6 all-reduce.4
  313.0 23.0 all-gather.4
  340.5 34.6 all-reduce.4
  378.9 23.0 all-gather.4
  406.5 34.6 all-reduce.4
  444.9 23.0 all-gather.4
  472.4 34.6 all-reduce.4
  510.5 23.0 all-gather.4
  538.0 34.6 all-reduce.4
  576.1 23.0 all-gather.4
  603.6 34.6 all-reduce.4
